TPU v7x, 32 devices: a whole 2x2x4 slice. The times are simulated.
32 devices in a mesh: fsdp: 4 (over y, x), tensor: 8 (over z, core).
Axes of the slice: x: 2, y: 2, z: 4, core: 2. Of those that a mesh axis runs over, the one named last changes fastest.
Arguments:
- block_input: bfloat16 [8, 1536, 1152], P('fsdp', 'tensor'), may hold values from -6 to 6
- segment_ids: int32 [8, 1536], P('fsdp'), may hold values from -1 to 15, as said below
- norm_gains: float32 [2, 1152], replicated, may hold values from 0.5 to 1.5
- row_biases: float32 [4, 1152], replicated, may hold values from -0.15 to 0.15
- in_projection: bfloat16 [3, 1152, 1152], P(None, 'fsdp', 'tensor'), may hold values from -0.1875 to 0.1875
- query_value_bias: float32 [2, 1152], P(None, 'tensor'), may hold values from -0.12 to 0.12
- out_projection: bfloat16 [1152, 1152], P('tensor', 'fsdp'), may hold values from -4 to 4
- up_weight: bfloat16 [1152, 4304], P('fsdp', 'tensor'), may hold values from -0.1875 to 0.1875
- unit_bias: bfloat16 [4304], P('tensor'), may hold values from -3 to 3
- down_weight: bfloat16 [4304, 1152], P('tensor', 'fsdp'), may hold values from -0.1875 to 0.1875
- cotangent: bfloat16 [8, 1536, 1152], P('fsdp', 'tensor'), may hold values from -6 to 6
Outputs:
- block_output: bfloat16 [8, 1536, 1152], P('fsdp', 'tensor')
- input_grad: float32 [8, 1536, 1152], P('fsdp', 'tensor')
- norm_gains_grad: float32 [2, 1152], replicated
- row_biases_grad: float32 [4, 1152], replicated
- in_projection_grad: float32 [3, 1152, 1152], P(None, 'fsdp', 'tensor')
- query_value_bias_grad: float32 [2, 1152], P(None, 'tensor')
- out_projection_grad: float32 [1152, 1152], P('tensor', 'fsdp')
- up_weight_grad: float32 [1152, 4304], P('fsdp', 'tensor')
- unit_bias_grad: float32 [4304], P('tensor')
- down_weight_grad: float32 [4304, 1152], P('tensor', 'fsdp')
Inputs may be any that keep to these rules, and one draw needn't show every extreme that they name: `segment_ids`: row block b holds 2 images in order; image j is a run of 729 consecutive rows with the id b * 2 + j, and every other row is padding with the id -1.
All inputs are finite; a program needn't handle non-finite values.
Results may differ from a plain program's by a relative error of at most 0.012.
Values may be sent and summed in bfloat16 or wider, within the bound.
A program may use at most 192 MiB of HBM per device.

v0:
```python
import jax
import jax.numpy as jnp
from jax import lax
from jax.sharding import PartitionSpec as P

DH = 72
IMG_MB = 2
EPS = 1e-06
GELU_C = 0.7978845608028654


def norm_forward(values, norm_gain, norm_shift):
    center = values - jnp.mean(values, axis=-1, keepdims=True)
    factor = lax.rsqrt(jnp.mean(center * center, axis=-1, keepdims=True) + EPS)
    scaled = center * factor
    return (scaled * norm_gain + norm_shift, scaled, factor)


def norm_backward(upstream, scaled, factor, norm_gain):
    inside = upstream * norm_gain
    return factor * (
        inside
        - jnp.mean(inside, axis=-1, keepdims=True)
        - scaled * jnp.mean(inside * scaled, axis=-1, keepdims=True)
    )


def gelu(pre_act):
    return (
        0.5
        * pre_act
        * (1.0 + jnp.tanh(GELU_C * (pre_act + 0.044715 * pre_act * pre_act * pre_act)))
    )


def gelu_back(pre_act, upstream):
    return jax.vjp(gelu, pre_act)[1](upstream)[0]


def product(left, right):
    return jnp.dot(left, right, preferred_element_type=jnp.float32)


def product_left_t(left, right):
    return lax.dot_general(
        left, right, (((0,), (0,)), ((), ())), preferred_element_type=jnp.float32
    )


def product_right_t(left, right):
    return lax.dot_general(
        left, right, (((1,), (1,)), ((), ())), preferred_element_type=jnp.float32
    )


def fetch_forward(in_projection, out_projection, up_weight, down_weight):
    return (
        lax.all_gather(in_projection, "fsdp", axis=1, tiled=True),
        lax.all_gather(out_projection, "fsdp", axis=1, tiled=True),
        lax.all_gather(up_weight, "fsdp", axis=0, tiled=True),
        lax.all_gather(down_weight, "fsdp", axis=1, tiled=True),
    )


def fetch_backward(in_projection, out_projection, up_weight, down_weight):
    return (
        lax.all_gather(in_projection, "fsdp", axis=1, tiled=True),
        lax.all_gather(out_projection, "fsdp", axis=1, tiled=True),
        lax.all_gather(up_weight, "fsdp", axis=0, tiled=True),
        lax.all_gather(down_weight, "fsdp", axis=1, tiled=True),
    )


def attend(queries, key_rows, value_rows, segments):
    rows_count, width = queries.shape
    heads = width // DH
    block = rows_count // IMG_MB
    score_scale = DH ** (-0.5)
    query_blocks = queries.reshape(IMG_MB, block, heads, DH)
    key_three = key_rows.reshape(rows_count, heads, DH)
    value_three = value_rows.reshape(rows_count, heads, DH)
    segment_blocks = segments.reshape(IMG_MB, block)

    def one_block(pieces):
        query_block, block_segments = pieces
        scores = (
            jnp.einsum("qhd,khd->hqk", query_block, key_three, preferred_element_type=jnp.float32)
            * score_scale
        )
        allowed_pairs = (block_segments[:, None] == segments[None, :])[None]
        log_total = jnp.log(
            jnp.sum(jnp.where(allowed_pairs, jnp.exp(scores), 0.0), axis=2, keepdims=True)
        )
        probs = jnp.where(allowed_pairs, jnp.exp(scores - log_total), 0.0).astype(jnp.bfloat16)
        context = jnp.einsum(
            "hqk,khd->qhd", probs, value_three, preferred_element_type=jnp.float32
        ).astype(jnp.bfloat16)
        return (context.reshape(block, width), log_total)

    context, log_total = lax.map(one_block, (query_blocks, segment_blocks))
    return (context.reshape(rows_count, width), log_total)


def attend_back(queries, key_rows, value_rows, context, context_grad, log_total, segments):
    rows_count, width = queries.shape
    heads = width // DH
    block = rows_count // IMG_MB
    score_scale = DH ** (-0.5)
    key_three = key_rows.reshape(rows_count, heads, DH)
    value_three = value_rows.reshape(rows_count, heads, DH)
    pieces = (
        queries.reshape(IMG_MB, block, heads, DH),
        context.reshape(IMG_MB, block, heads, DH),
        context_grad.reshape(IMG_MB, block, heads, DH),
        log_total,
        segments.reshape(IMG_MB, block),
    )

    def one_block(carry, piece):
        key_acc, value_acc = carry
        query_block, context_block, back_block, total_block, block_segments = piece
        scores = (
            jnp.einsum("qhd,khd->hqk", query_block, key_three, preferred_element_type=jnp.float32)
            * score_scale
        )
        allowed_pairs = (block_segments[:, None] == segments[None, :])[None]
        exact = jnp.where(allowed_pairs, jnp.exp(scores - total_block), 0.0)
        probs = exact.astype(jnp.bfloat16)
        value_acc = value_acc + jnp.einsum(
            "hqk,qhd->khd", probs, back_block, preferred_element_type=jnp.float32
        )
        prob_grad = jnp.einsum(
            "qhd,khd->hqk", back_block, value_three, preferred_element_type=jnp.float32
        )
        delta = jnp.einsum(
            "qhd,qhd->hq", back_block, context_block, preferred_element_type=jnp.float32
        )[:, :, None]
        score_grad = (exact * (prob_grad - delta) * score_scale).astype(jnp.bfloat16)
        query_grad = jnp.einsum(
            "hqk,khd->qhd", score_grad, key_three, preferred_element_type=jnp.float32
        )
        key_acc = key_acc + jnp.einsum(
            "hqk,qhd->khd", score_grad, query_block, preferred_element_type=jnp.float32
        )
        return ((key_acc, value_acc), query_grad.reshape(block, width))

    zeros = jnp.zeros((rows_count, heads, DH), jnp.float32)
    (key_grad, value_grad), query_grad = lax.scan(one_block, (zeros, zeros), pieces)
    return (
        query_grad.reshape(rows_count, width),
        key_grad.reshape(rows_count, width),
        value_grad.reshape(rows_count, width),
    )


def on_device(
    block_input,
    segment_ids,
    norm_gains,
    row_biases,
    in_projection,
    query_value_bias,
    out_projection,
    up_weight,
    unit_bias,
    down_weight,
    cotangent,
):
    batches = block_input.shape[0]
    model_width = block_input.shape[2]
    head_cols = in_projection.shape[2]
    unit_cols = up_weight.shape[1]
    tensor_count = lax.axis_size("tensor")
    gains_sum = jnp.zeros((2, model_width), jnp.float32)
    shifts_sum = jnp.zeros((4, model_width), jnp.float32)
    in_sum = jnp.zeros((3, model_width, head_cols), jnp.float32)
    bias_sum = jnp.zeros((2, head_cols), jnp.float32)
    out_sum = jnp.zeros((head_cols, model_width), jnp.float32)
    up_sum = jnp.zeros((model_width, unit_cols), jnp.float32)
    down_sum = jnp.zeros((unit_cols, model_width), jnp.float32)
    unit_sum = jnp.zeros((unit_cols,), jnp.float32)
    output_list = []
    grad_list = []
    for batch in range(batches):
        rows_in = block_input[batch]
        segments = segment_ids[batch]
        grad_rows = cotangent[batch]
        in_whole, out_whole, up_whole, down_whole = fetch_forward(
            in_projection, out_projection, up_weight, down_weight
        )
        input_float = rows_in.astype(jnp.float32)
        first_out, first_scaled, first_factor = norm_forward(
            input_float, norm_gains[0], row_biases[0]
        )
        first_norm = first_out.astype(jnp.bfloat16)
        first_full = lax.all_gather(first_norm, "tensor", axis=0, tiled=True)
        projected = jnp.einsum(
            "rd,kdx->krx", first_full, in_whole, preferred_element_type=jnp.float32
        )
        queries = (projected[0] + query_value_bias[0]).astype(jnp.bfloat16)
        key_rows = projected[1].astype(jnp.bfloat16)
        value_rows = (projected[2] + query_value_bias[1]).astype(jnp.bfloat16)
        context, log_total = attend(queries, key_rows, value_rows, segments)
        attention_part = lax.psum_scatter(
            product(context, out_whole), "tensor", scatter_dimension=0, tiled=True
        )
        residual = input_float + attention_part + row_biases[2]
        second_out, second_scaled, second_factor = norm_forward(
            residual, norm_gains[1], row_biases[1]
        )
        second_norm = second_out.astype(jnp.bfloat16)
        upstream = grad_rows.astype(jnp.float32)
        second_full = lax.all_gather(second_norm, "tensor", axis=0, tiled=True)
        pre_act = product(second_full, up_whole) + unit_bias
        hidden = gelu(pre_act).astype(jnp.bfloat16)
        unit_part = lax.psum_scatter(
            product(hidden, down_whole).astype(jnp.bfloat16),
            "tensor",
            scatter_dimension=0,
            tiled=True,
        ).astype(jnp.float32)
        output_list.append((residual + unit_part + row_biases[3]).astype(jnp.bfloat16))
        in_whole, out_whole, up_whole, down_whole = fetch_backward(
            in_projection, out_projection, up_weight, down_weight
        )
        grad_full = lax.all_gather(grad_rows, "tensor", axis=0, tiled=True)
        down_sum = down_sum + product_left_t(hidden, grad_full)
        pre_grad = gelu_back(pre_act, product_right_t(grad_full, down_whole))
        pre_half = pre_grad.astype(jnp.bfloat16)
        unit_sum = unit_sum + jnp.sum(pre_grad, axis=0)
        up_sum = up_sum + product_left_t(second_full, pre_half)
        second_grad = lax.psum_scatter(
            product_right_t(pre_half, up_whole), "tensor", scatter_dimension=0, tiled=True
        )
        residual_grad = upstream + norm_backward(
            second_grad, second_scaled, second_factor, norm_gains[1]
        )
        residual_half = residual_grad.astype(jnp.bfloat16)
        residual_full = lax.all_gather(residual_half, "tensor", axis=0, tiled=True)
        out_sum = out_sum + product_left_t(context, residual_full)
        context_grad = product_right_t(residual_full, out_whole).astype(jnp.bfloat16)
        query_grad, key_grad, value_grad = attend_back(
            queries, key_rows, value_rows, context, context_grad, log_total, segments
        )
        bias_sum = bias_sum + jnp.stack([jnp.sum(query_grad, axis=0), jnp.sum(value_grad, axis=0)])
        triple_half = jnp.stack(
            [
                query_grad.astype(jnp.bfloat16),
                key_grad.astype(jnp.bfloat16),
                value_grad.astype(jnp.bfloat16),
            ]
        )
        in_sum = in_sum + jnp.einsum(
            "rd,krx->kdx", first_full, triple_half, preferred_element_type=jnp.float32
        )
        first_grad = lax.psum_scatter(
            jnp.einsum("krx,kdx->rd", triple_half, in_whole, preferred_element_type=jnp.float32),
            "tensor",
            scatter_dimension=0,
            tiled=True,
        )
        grad_list.append(
            residual_grad + norm_backward(first_grad, first_scaled, first_factor, norm_gains[0])
        )
        gains_sum = gains_sum + jnp.stack(
            [
                jnp.sum(first_grad * first_scaled, axis=0),
                jnp.sum(second_grad * second_scaled, axis=0),
            ]
        )
        shifts_sum = shifts_sum + jnp.stack(
            [
                jnp.sum(first_grad, axis=0),
                jnp.sum(second_grad, axis=0),
                jnp.sum(residual_grad, axis=0),
                jnp.sum(upstream, axis=0),
            ]
        )
    in_grad, out_grad, up_grad, down_grad = (
        lax.psum_scatter(in_sum, "fsdp", scatter_dimension=1, tiled=True),
        lax.psum_scatter(out_sum, "fsdp", scatter_dimension=1, tiled=True),
        lax.psum_scatter(up_sum, "fsdp", scatter_dimension=0, tiled=True),
        lax.psum_scatter(down_sum, "fsdp", scatter_dimension=1, tiled=True),
    )
    tensor_index = lax.axis_index("tensor")
    bias_wide = lax.dynamic_update_slice(
        jnp.zeros((2, head_cols * tensor_count), jnp.float32),
        bias_sum,
        (jnp.int32(0), tensor_index * head_cols),
    )
    unit_wide = lax.dynamic_update_slice(
        jnp.zeros((unit_cols * tensor_count,), jnp.float32), unit_sum, (tensor_index * unit_cols,)
    )
    gains_total, shifts_total, bias_total, unit_total = lax.psum(
        (gains_sum, shifts_sum, bias_wide, unit_wide), ("fsdp", "tensor")
    )
    bias_grad = lax.dynamic_slice_in_dim(bias_total, tensor_index * head_cols, head_cols, 1)
    unit_grad = lax.dynamic_slice_in_dim(unit_total, tensor_index * unit_cols, unit_cols, 0)
    return (
        jnp.stack(output_list),
        jnp.stack(grad_list),
        gains_total,
        shifts_total,
        in_grad,
        bias_grad,
        out_grad,
        up_grad,
        unit_grad,
        down_grad,
    )


def solution(mesh):
    return jax.shard_map(
        on_device,
        mesh=mesh,
        in_specs=(
            P("fsdp", "tensor", None),
            P("fsdp", None),
            P(),
            P(),
            P(None, "fsdp", "tensor"),
            P(None, "tensor"),
            P("tensor", "fsdp"),
            P("fsdp", "tensor"),
            P("tensor"),
            P("tensor", "fsdp"),
            P("fsdp", "tensor", None),
        ),
        out_specs=(
            P("fsdp", "tensor", None),
            P("fsdp", "tensor", None),
            P(),
            P(),
            P(None, "fsdp", "tensor"),
            P(None, "tensor"),
            P("tensor", "fsdp"),
            P("fsdp", "tensor"),
            P("tensor"),
            P("tensor", "fsdp"),
        ),
        check_vma=False,
    )
```

profile of v0, /device:TPU:0, one launch (start us, length us, event | category | flops | bytes accessed | tf_op | source)
XLA Modules:
  0.0 1204.3 jit_solution(9622381354068464262)
XLA Ops:
  18.8 11.3 all-gather.2
  31.6 21.0 %all_gather.49 = bf16[3,1152,144]{2,0,1:T(4,128)(2,1)S(1)} all-gather(bf16[3,288,144]{2,0,1:T(4,128)(2,1)S(1)} %copy.40), channel_id=1, replica_groups=mesh['fsdp'=4,'tensor'=8] {'fsdp'}, dimensions={1}, use_global_device_ids=true | all-gather | bytes 1244160 | tf_op jit(solution)/shard_map/all_gather | solution.py:58
  52.6 3.2 copy.41
  55.8 5.0 all-gather.14.cloned.1.call-done
  60.8 4.2 fusion.173
  65.2 38.2 %all-gather.22.cloned.1.call-done = bf16[1536,1152]{1,0:T(8,128)(2,1)} async-done(((bf16[192,1152]{1,0:T(8,128)(2,1)}), bf16[1536,1152]{1,0:T(8,128)(2,1)}) %all-gather.22.cloned.1.call-update) | async-done | bytes 3538960 | tf_op jit(solution)/shard_map/all_gather | solution.py:196
  103.4 3.9 fusion.175
  116.7 13.7 %while.54 = (s32[]{:T(128)}, bf16[2,768,144]{1,2,0:T(8,128)(2,1)S(1)}, f32[2,2,768,1]{2,1,3,0:T(2,128)S(1)}, s32[2,768]{1,0:T(2,128)S(1)}, s32[1,1536]{1,0:T(1,1...) while((s32[]{:T(128)}, ...), condition=%wide.region_4.5_spmd, body=%wide.region_2.4_spmd.sunk | while | flops 697281024 | bytes 24247424 | solution.py:100
  117.5 3.1 select_reduce_fusion.4
  120.6 2.8 fusion.262
  124.3 3.1 select_reduce_fusion.4
  127.5 2.8 fusion.262
  131.2 4.2 fusion.174
  137.4 13.8 %while.55 = (s32[]{:T(128)}, bf16[2,768,144]{1,2,0:T(8,128)(2,1)S(1)}, f32[2,2,768,1]{2,1,3,0:T(2,128)S(1)}, s32[2,768]{1,0:T(2,128)S(1)}, s32[1,1536]{1,0:T(1,1...) while((s32[]{:T(128)}, ...), condition=%wide.region_13.14_spmd, body=%wide.region_11.13_spmd.sunk | while | flops 697281024 | bytes 24247424 | solution.py:100
  138.2 3.1 select_reduce_fusion.5
  141.3 2.9 fusion.265
  145.0 3.1 select_reduce_fusion.5
  148.2 2.9 fusion.265
  151.2 4.2 fusion.176
  156.1 55.4 %reduce-scatter.17.cloned.1.call-done = f32[192,1152]{1,0:T(8,128)} async-done(((f32[1536,1152]{1,0:T(8,128)}), f32[192,1152]{1,0:T(8,128)}) %reduce-scatter.17.cloned.1.call-update) | async-done | bytes 884752 | tf_op jit(solution)/shard_map/reduce_scatter | solution.py:204
  211.6 77.8 %reduce-scatter.21.cloned.1.call-done = f32[192,1152]{1,0:T(8,128)} async-done(((f32[1536,1152]{1,0:T(8,128)}), f32[192,1152]{1,0:T(8,128)}) %reduce-scatter.21.cloned.1.call-update) | async-done | bytes 884752 | tf_op jit(solution)/shard_map/reduce_scatter | solution.py:204
  298.3 35.3 %all-gather.24.cloned.1.call-done = bf16[1536,1152]{1,0:T(8,128)(2,1)} async-done(((bf16[192,1152]{1,0:T(8,128)(2,1)}), bf16[1536,1152]{1,0:T(8,128)(2,1)}) %all-gather.24.cloned.1.call-update) | async-done | bytes 3538960 | tf_op jit(solution)/shard_map/all_gather | solution.py:213
  333.6 6.5 convolution_add_fusion.2
  340.1 24.0 %all-gather.20.cloned.1.call-done = bf16[538,1152]{0,1:T(8,128)(2,1)} async-done(((bf16[538,288]{0,1:T(8,128)(2,1)}), bf16[538,1152]{0,1:T(8,128)(2,1)}) %all-gather.20.cloned.1.call-update) | async-done | bytes 1239568 | tf_op jit(solution)/shard_map/all_gather | solution.py:61
  364.1 43.6 %all-gather.32.cloned.1.call-done = bf16[1,1536,1152]{2,1,0:T(8,128)(2,1)} async-done(((bf16[1,192,1152]{2,1,0:T(8,128)(2,1)}), bf16[1,1536,1152]{2,1,0:T(8,128)(2,1)}) %all-gather.32.cloned.1.call-update) | async-done | bytes 3538960 | tf_op jit(solution)/shard_map/all_gather | solution.py:226
  407.7 9.2 fusion.170
  418.1 5.3 fusion.142
  423.7 26.5 %all-gather.16.cloned.1.call-done = bf16[1536,1152]{1,0:T(8,128)(2,1)} async-done(((bf16[192,1152]{1,0:T(8,128)(2,1)}), bf16[1536,1152]{1,0:T(8,128)(2,1)}) %all-gather.16.cloned.1.call-update) | async-done | bytes 3538960 | tf_op jit(solution)/shard_map/all_gather | solution.py:213
  450.2 6.6 convolution_add_fusion.3
  456.8 35.9 %all-gather.30.cloned.1.call-done = bf16[1,1536,1152]{2,1,0:T(8,128)(2,1)} async-done(((bf16[1,192,1152]{2,1,0:T(8,128)(2,1)}), bf16[1,1536,1152]{2,1,0:T(8,128)(2,1)}) %all-gather.30.cloned.1.call-update) | async-done | bytes 3538960 | tf_op jit(solution)/shard_map/all_gather | solution.py:226
  492.7 9.2 fusion.169
  503.0 5.4 fusion.146
  508.9 7.7 convolution_convert_fusion.1
  516.6 7.7 convolution_convert_fusion
  524.3 46.4 %reduce-scatter.29.cloned.1.call-done = f32[192,1152]{1,0:T(8,128)} async-done(((f32[1536,1152]{1,0:T(8,128)}), f32[192,1152]{1,0:T(8,128)}) %reduce-scatter.29.cloned.1.call-update) | async-done | bytes 884752 | tf_op jit(solution)/shard_map/reduce_scatter | solution.py:232
  570.8 77.7 %reduce-scatter.25.cloned.1.call-done = f32[192,1152]{1,0:T(8,128)} async-done(((f32[1536,1152]{1,0:T(8,128)}), f32[192,1152]{1,0:T(8,128)}) %reduce-scatter.25.cloned.1.call-update) | async-done | bytes 884752 | tf_op jit(solution)/shard_map/reduce_scatter | solution.py:232
  653.5 39.3 %reduce-scatter.19.cloned.1.call-done = bf16[192,1152]{1,0:T(8,128)(2,1)} async-done(((bf16[1536,1152]{1,0:T(8,128)(2,1)}), bf16[192,1152]{1,0:T(8,128)(2,1)}) %reduce-scatter.19.cloned.1.call-update) | async-done | bytes 442384 | tf_op jit(solution)/shard_map/reduce_scatter | solution.py:216
  692.9 44.4 %reduce-scatter.23.cloned.1.call-done = bf16[192,1152]{1,0:T(8,128)(2,1)} async-done(((bf16[1536,1152]{1,0:T(8,128)(2,1)}), bf16[192,1152]{1,0:T(8,128)(2,1)}) %reduce-scatter.23.cloned.1.call-update) | async-done | bytes 442384 | tf_op jit(solution)/shard_map/reduce_scatter | solution.py:216
  737.3 4.4 fusion.156
  745.9 37.8 %all-gather.26.cloned.1.call-done = bf16[1536,1152]{1,0:T(8,128)(2,1)} async-done(((bf16[192,1152]{1,0:T(8,128)(2,1)}), bf16[1536,1152]{1,0:T(8,128)(2,1)}) %all-gather.26.cloned.1.call-update) | async-done | bytes 3538960 | tf_op jit(solution)/shard_map/all_gather | solution.py:239
  783.7 3.3 convolution_convert_fusion.3
  789.9 40.6 %while.56 = (s32[]{:T(128)}, f32[1536,2,72]{0,2,1:T(8,128)S(1)}, f32[1536,2,72]{0,2,1:T(8,128)}, f32[2,768,144]{1,2,0:T(8,128)}, bf16[2,768,2,72]{1,3,2,0:T(8,12...) while((s32[]{:T(128)}, f32[1536,2,72]{0,2,1:T(8,128)S(1)}, ...), condition=%wide.region_22.23_spmd.clone, body=%wide.region_21.22_spmd.clone.sunk | while | flops 1727150592 | bytes 81067536 | solution.py:148
  802.3 4.1 multiply_convert_fusion.10
  819.8 2.8 fusion.278
  822.6 4.1 multiply_convert_fusion.10
  830.6 3.4 convolution_convert_fusion.2
  835.1 37.9 %while.57 = (s32[]{:T(128)}, f32[1536,2,72]{0,2,1:T(8,128)S(1)}, f32[1536,2,72]{0,2,1:T(8,128)}, f32[2,768,144]{1,2,0:T(8,128)}, bf16[2,768,2,72]{1,3,2,0:T(8,12...) while((s32[]{:T(128)}, f32[1536,2,72]{0,2,1:T(8,128)S(1)}, ...), condition=%wide.region_30.31_spmd.clone, body=%wide.region_29.30_spmd.clone.sunk | while | flops 1727150592 | bytes 77491600 | solution.py:148
  846.4 4.1 multiply_convert_fusion.11
  862.3 2.8 fusion.292
  865.1 4.1 multiply_convert_fusion.11
  872.9 3.0 fusion.177
  891.3 4.0 copy.70
  895.2 6.3 reshape.415
  901.6 5.2 convolution_bitcast_fusion.3
  908.0 5.2 convolution_bitcast_fusion.2
  913.3 5.6 fusion.144
  919.0 4.8 convolution_add_fusion.1
  924.1 6.6 fusion.77
  930.7 4.8 convolution_add_fusion
  940.4 8.0 reduce-scatter.37.cloned.1.call-done
  953.4 74.2 %reduce-scatter.27.cloned.1.call-done = f32[192,1152]{1,0:T(8,128)} async-done(((f32[1536,1152]{1,0:T(8,128)}), f32[192,1152]{1,0:T(8,128)}) %reduce-scatter.27.cloned.1.call-update) | async-done | bytes 884752 | tf_op jit(solution)/shard_map/reduce_scatter | solution.py:256
  1027.6 77.9 %reduce-scatter.31.cloned.1.call-done = f32[192,1152]{1,0:T(8,128)} async-done(((f32[1536,1152]{1,0:T(8,128)}), f32[192,1152]{1,0:T(8,128)}) %reduce-scatter.31.cloned.1.call-update) | async-done | bytes 884752 | tf_op jit(solution)/shard_map/reduce_scatter | solution.py:256
  1108.0 39.9 %all-reduce = (f32[2,1152]{1,0:T(2,128)}, f32[4,1152]{1,0:T(4,128)}, f32[2,1152]{1,0:T(2,128)S(1)}, f32[4304]{0:T(1024)S(1)}) all-reduce(f32[2,1152]{1,0:T(2,128)S(1)} %maximum_add_fusion.1, f32[4,1152]{1,0:T(4,128)S(1)} %maximum_add_fusion, ...), channel_id=1, replica_groups=mesh['fsdp'=4,'tensor'=8] {'fsdp','tensor'}, use_global_device_ids=true, to_apply=%region_38.39 | all-reduce | flops 13520 | bytes 108160 | tf_op jit(solution)/shard_map/psum | solution.py:294
  1152.6 43.9 %reduce-scatter.35.cloned.1.call-done = f32[538,288]{0,1:T(8,128)} async-done(((f32[538,1152]{0,1:T(8,128)}), f32[538,288]{0,1:T(8,128)}) %reduce-scatter.35.cloned.1.call-update) | async-done | bytes 619792 | tf_op jit(solution)/shard_map/reduce_scatter | solution.py:283
  (480 shorter events, 142.2 us)
Async XLA Ops:
  8.0 9.3 copy-start.91
  8.0 9.5 copy-start.88
  8.0 10.7 copy-start.68
  8.0 23.2 %copy-start.57 = (bf16[3,288,144]{1,2,0:T(8,128)(2,1)S(1)}, bf16[3,288,144]{1,2,0:T(8,128)(2,1)}, u32[]{:S(2)}) copy-start(bf16[3,288,144]{1,2,0:T(8,128)(2,1)} %param.23) | copy-start | bytes 746500
  8.1 52.8 %all-gather.14.cloned.1.call-start = ((), (), s32[]{:S(2)}) async-start(), calls=%async_computation.12 | async-start | bytes 3981312 | tf_op jit(solution)/shard_map/all_gather | solution.py:196
  9.5 9.2 copy-start.76
  9.5 9.2 copy-start.78
  11.1 7.7 copy-start.82
  11.1 7.7 copy-start.84
  12.5 6.3 copy-start.65
  16.5 86.9 %all-gather.22.cloned.1.call-start = ((), (), s32[]{:S(2)}) async-start(), calls=%async_computation.18 | async-start | bytes 3981312 | tf_op jit(solution)/shard_map/all_gather | solution.py:196
  17.3 194.3 %reduce-scatter.17.cloned.1.call-start = ((), (), s32[]{:S(2)}) async-start(), calls=%async_computation.13 | async-start | bytes 7962624 | tf_op jit(solution)/shard_map/reduce_scatter | solution.py:204
  65.0 38.4 %copy-start.34 = (bf16[3,1152,144]{1,2,0:T(8,128)(2,1)S(1)}, bf16[3,1152,144]{1,2,0:T(8,128)(2,1)}, u32[]{:S(2)}) copy-start(bf16[3,1152,144]{1,2,0:T(8,128)(2,1)} %copy.41) | copy-start | bytes 2985988
  116.7 14.5 %copy-start.29 = (bf16[1152,144]{0,1:T(8,128)(2,1)S(1)}, bf16[1152,144]{0,1:T(8,128)(2,1)}, u32[]{:S(2)}) copy-start(bf16[1152,144]{0,1:T(8,128)(2,1)} %reshape.400) | copy-start | bytes 995332
  130.4 5.0 copy-start.6
  130.4 5.0 copy-start.64
  135.4 154.0 %reduce-scatter.21.cloned.1.call-start = ((), (), s32[]{:S(2)}) async-start(), calls=%async_computation.19 | async-start | bytes 7962624 | tf_op jit(solution)/shard_map/reduce_scatter | solution.py:204
  151.1 4.3 copy-start
  151.1 4.3 copy-start.4
  151.1 4.3 copy-start.8
  155.5 133.9 %copy-start.2 = (bf16[2,192,1152]{2,1,0:T(8,128)(2,1)S(1)}, bf16[2,192,1152]{2,1,0:T(8,128)(2,1)}, u32[]{:S(2)}) copy-start(bf16[2,192,1152]{2,1,0:T(8,128)(2,1)} %param.19) | copy-start | bytes 2654212
  155.5 136.2 %copy-start.67 = (f32[1152]{0:T(1024)S(1)}, f32[1152]{0:T(1024)}, u32[]{:S(2)}) copy-start(f32[1152]{0:T(1024)} %get-tuple-element.414) | copy-start | bytes 13828
  155.5 142.8 %all-gather.18.cloned.1.call-start = ((), (), s32[]{:S(2)}) async-start(), calls=%async_computation.15 | async-start | bytes 1843200 | tf_op jit(solution)/shard_map/all_gather | solution.py:60
  156.1 177.5 %all-gather.24.cloned.1.call-start = ((), (), s32[]{:S(2)}) async-start(), calls=%async_computation.20 | async-start | bytes 3981312 | tf_op jit(solution)/shard_map/all_gather | solution.py:213
  293.7 70.4 %all-gather.20.cloned.1.call-start = ((), (), s32[]{:S(2)}) async-start(), calls=%async_computation.16 | async-start | bytes 1843200 | tf_op jit(solution)/shard_map/all_gather | solution.py:61
  294.3 113.4 %all-gather.32.cloned.1.call-start = ((), (), s32[]{:S(2)}) async-start(), calls=%async_computation.31 | async-start | bytes 3981312 | tf_op jit(solution)/shard_map/all_gather | solution.py:226
  295.4 154.8 %all-gather.16.cloned.1.call-start = ((), (), s32[]{:S(2)}) async-start(), calls=%async_computation.14 | async-start | bytes 3981312 | tf_op jit(solution)/shard_map/all_gather | solution.py:213
  296.1 196.5 %all-gather.30.cloned.1.call-start = ((), (), s32[]{:S(2)}) async-start(), calls=%async_computation.30 | async-start | bytes 3981312 | tf_op jit(solution)/shard_map/all_gather | solution.py:226
  296.8 274.0 %reduce-scatter.29.cloned.1.call-start = ((), (), s32[]{:S(2)}) async-start(), calls=%async_computation.25 | async-start | bytes 7962624 | tf_op jit(solution)/shard_map/reduce_scatter | solution.py:232
  407.7 10.4 copy-start.96
  423.4 225.1 %reduce-scatter.25.cloned.1.call-start = ((), (), s32[]{:S(2)}) async-start(), calls=%async_computation.22 | async-start | bytes 7962624 | tf_op jit(solution)/shard_map/reduce_scatter | solution.py:232
  492.7 10.4 copy-start.97
  508.4 184.5 %reduce-scatter.19.cloned.1.call-start = ((), (), s32[]{:S(2)}) async-start(), calls=%async_computation.17 | async-start | bytes 3981312 | tf_op jit(solution)/shard_map/reduce_scatter | solution.py:216
  516.6 220.8 %reduce-scatter.23.cloned.1.call-start = ((), (), s32[]{:S(2)}) async-start(), calls=%async_computation.21 | async-start | bytes 3981312 | tf_op jit(solution)/shard_map/reduce_scatter | solution.py:216
  524.3 259.4 %all-gather.26.cloned.1.call-start = ((), (), s32[]{:S(2)}) async-start(), calls=%async_computation.23 | async-start | bytes 3981312 | tf_op jit(solution)/shard_map/all_gather | solution.py:239
  741.8 41.9 %copy-start.30 = (bf16[1152,144]{0,1:T(8,128)(2,1)S(1)}, bf16[1152,144]{0,1:T(8,128)(2,1)}, u32[]{:S(2)}) copy-start(bf16[1152,144]{0,1:T(8,128)(2,1)} %reshape.400) | copy-start | bytes 995332
  743.5 87.0 %all-gather.28.cloned.1.call-start = ((), (), s32[]{:S(2)}) async-start(), calls=%async_computation.26 | async-start | bytes 3981312 | tf_op jit(solution)/shard_map/all_gather | solution.py:239
  745.6 193.0 %reduce-scatter.39.cloned.1.call-start = ((), (), s32[]{:S(2)}) async-start(), calls=%async_computation.33 | async-start | bytes 1474560
  830.5 4.5 copy-start.1
  830.5 4.5 copy-start.42
  830.5 4.5 copy-start.60
  830.5 4.5 copy-start.63
  876.3 4.3 copy-start.25
  880.4 68.0 %reduce-scatter.37.cloned.1.call-start = ((), (), s32[]{:S(2)}) async-start(), calls=%async_computation.32 | async-start | bytes 2949120
  883.7 5.5 copy-start.47
  884.4 4.8 copy-start.49
  895.2 6.4 copy-start.35
  895.2 6.4 copy-start.55
  901.5 126.1 %reduce-scatter.27.cloned.1.call-start = ((), (), s32[]{:S(2)}) async-start(), calls=%async_computation.24 | async-start | bytes 7962624 | tf_op jit(solution)/shard_map/reduce_scatter | solution.py:256
  906.8 198.8 %reduce-scatter.31.cloned.1.call-start = ((), (), s32[]{:S(2)}) async-start(), calls=%async_computation.27 | async-start | bytes 7962624 | tf_op jit(solution)/shard_map/reduce_scatter | solution.py:256
  913.3 5.7 copy-start.99
  913.3 239.3 %reduce-scatter.33.cloned.1.call-start = ((), (), s32[]{:S(2)}) async-start(), calls=%async_computation.28 | async-start | bytes 3686400 | tf_op jit(solution)/shard_map/reduce_scatter | solution.py:282
  913.3 5.7 copy-start.94
  923.8 272.6 %reduce-scatter.35.cloned.1.call-start = ((), (), s32[]{:S(2)}) async-start(), calls=%async_computation.29 | async-start | bytes 3686400 | tf_op jit(solution)/shard_map/reduce_scatter | solution.py:283
  924.1 6.6 copy-start.95
  924.1 6.6 copy-start.101
  936.7 168.9 %copy-start.3 = (bf16[2,192,1152]{2,1,0:T(8,128)(2,1)S(1)}, bf16[2,192,1152]{2,1,0:T(8,128)(2,1)}, u32[]{:S(2)}) copy-start(bf16[2,192,1152]{2,1,0:T(8,128)(2,1)} %param.19) | copy-start | bytes 2654212
  936.7 168.9 %copy-start.66 = (f32[1152]{0:T(1024)S(1)}, f32[1152]{0:T(1024)}, u32[]{:S(2)}) copy-start(f32[1152]{0:T(1024)} %copy-done.65) | copy-start | bytes 13828
  936.7 168.9 %copy-start.77 = (f32[192]{0:T(256)S(1)}, f32[192]{0:T(256)}, u32[]{:S(2)}) copy-start(f32[192]{0:T(256)} %copy-done.76) | copy-start | bytes 2308
  936.7 168.9 %copy-start.79 = (f32[192]{0:T(256)S(1)}, f32[192]{0:T(256)}, u32[]{:S(2)}) copy-start(f32[192]{0:T(256)} %copy-done.78) | copy-start | bytes 2308
  936.7 168.9 %copy-start.83 = (f32[192]{0:T(256)S(1)}, f32[192]{0:T(256)}, u32[]{:S(2)}) copy-start(f32[192]{0:T(256)} %copy-done.82) | copy-start | bytes 2308
  936.7 168.9 %copy-start.85 = (f32[192]{0:T(256)S(1)}, f32[192]{0:T(256)}, u32[]{:S(2)}) copy-start(f32[192]{0:T(256)} %copy-done.84) | copy-start | bytes 2308
  940.4 208.8 %copy-start.14 = (f32[192,1152]{1,0:T(8,128)S(1)}, f32[192,1152]{1,0:T(8,128)}, u32[]{:S(2)}) copy-start(f32[192,1152]{1,0:T(8,128)} %copy-done.13) | copy-start | bytes 2654212
  940.4 208.8 %copy-start.15 = (f32[192,1152]{1,0:T(8,128)S(1)}, f32[192,1152]{1,0:T(8,128)}, u32[]{:S(2)}) copy-start(f32[192,1152]{1,0:T(8,128)} %get-tuple-element.523) | copy-start | bytes 2654212
  (80 other events, 177.6 us)
Sparse Core Ops, SparseCore 0:
  16.6 44.1 all-gather.13
  63.1 40.2 all-gather.21
  135.5 75.9 reduce-scatter.16
  213.7 75.6 reduce-scatter.20
  743.7 39.9 all-gather.25
  785.7 40.2 all-gather.27
Sparse Core Ops, SparseCore 1:
  157.8 28.7 all-gather.17
  293.8 39.8 all-gather.23
  335.3 28.8 all-gather.19
  366.4 41.3 all-gather.31
  410.0 40.2 all-gather.15
  452.4 40.2 all-gather.29
  494.8 75.9 reduce-scatter.28
  573.0 75.5 reduce-scatter.24
  650.7 42.1 reduce-scatter.18
  695.2 42.0 reduce-scatter.22
  880.4 27.5 reduce-scatter.38
  911.1 37.2 reduce-scatter.36
  950.6 77.0 reduce-scatter.26
  1030.0 75.5 reduce-scatter.30
  1109.2 41.4 reduce-scatter.32
  1154.3 42.0 reduce-scatter.34
where the time goes:
time: 1210 us; the launch traced here: 1200 us
  waiting for transfers between devices  795 us (66%)
  matrix products  193 us (16%)
  blocking collectives  72.1 us (6%)
  local copies, waits for them, and re-layouts  71.9 us (6%)
  other arithmetic  50.8 us (4%)
  between operations  17.5 us (1%)
    reduce_scatter x2, waiting for transfers between devices, on_device(): lax.psum_scatter(jnp.einsum('krx,kdx->rd', triple_half, in_whole, preferr...  152 us
    reduce_scatter x2, waiting for transfers between devices, on_device(): lax.psum_scatter(product(context, out_whole), 'tensor', scatter_dimension...  133 us
    reduce_scatter x2, waiting for transfers between devices, on_device(): lax.psum_scatter(product_right_t(pre_half, up_whole), 'tensor', scatter_d...  124 us
    reduce_scatter x2, waiting for transfers between devices, on_device(): lax.psum_scatter(product(hidden, down_whole).astype(jnp.bfloat16), 'tenso...  83.8 us
    all_gather x2, waiting for transfers between devices, on_device(): grad_full = lax.all_gather(grad_rows, 'tensor', axis=0, tiled=True)  79.5 us
    all_gather x2, waiting for transfers between devices, on_device(): second_full = lax.all_gather(second_norm, 'tensor', axis=0, tiled=True)  61.7 us
    reduce_scatter x1, waiting for transfers between devices, on_device(): lax.psum_scatter(down_sum, 'fsdp', scatter_dimension=1, tiled=True)  43.9 us
    all_gather x2, waiting for transfers between devices, on_device(): first_full = lax.all_gather(first_norm, 'tensor', axis=0, tiled=True)  43.2 us
  transfers between devices with their start and end apart: 22, of which 18 were waited for; matrix products, arithmetic and copies ran while one was open for 18% of the time, Pallas kernels for 0%

commit v1 on v0

--- a/solution.py
+++ b/solution.py
@@ -210,7 +210,10 @@
         )
         second_norm = second_out.astype(jnp.bfloat16)
         upstream = grad_rows.astype(jnp.float32)
-        second_full = lax.all_gather(second_norm, "tensor", axis=0, tiled=True)
+        second_full = jnp.concatenate(
+            lax.all_to_all(jnp.stack([second_norm] * lax.axis_size("tensor")), "tensor", 0, 0),
+            axis=0,
+        )
         pre_act = product(second_full, up_whole) + unit_bias
         hidden = gelu(pre_act).astype(jnp.bfloat16)
         unit_part = lax.psum_scatter(

time: 1210 us -> 1250 us (1.033)
  blocking collectives: 72.1 us -> 207 us
  waiting for transfers between devices: 795 us -> 698 us
    all_to_all x0 -> x1, blocking collectives: none -> 135 us  [on_device(): lax.all_to_all(jnp.stack([second_norm] * lax.axis_size('tensor')), 'tenso...]
    all_to_all x0 -> x1, waiting for transfers between devices: none -> 107 us  [on_device(): lax.all_to_all(jnp.stack([second_norm] * lax.axis_size('tensor')), 'tenso...]
    all_gather x2, waiting for transfers between devices: 79.5 us -> 0.01 us  [on_device(): grad_full = lax.all_gather(grad_rows, 'tensor', axis=0, tiled=True)]
    reduce_scatter x2, waiting for transfers between devices: 124 us -> 60.4 us  [on_device(): lax.psum_scatter(product_right_t(pre_half, up_whole), 'tensor', scatter_d...]
    all_gather x2 -> x0, waiting for transfers between devices: 61.7 us -> none  [on_device(): second_full = lax.all_gather(second_norm, 'tensor', axis=0, tiled=True)]
    reduce_scatter x2, waiting for transfers between devices: 133 us -> 160 us  [on_device(): lax.psum_scatter(product(context, out_whole), 'tensor', scatter_dimension...]
    all_gather x1, waiting for transfers between devices: 24 us -> 0.01 us  [fetch_forward(): lax.all_gather(down_weight, 'fsdp', axis=1, tiled=True)]
    unnamed x174 -> x184, local copies, waits for them, and re-layouts: 31.6 us -> 34.7 us
  transfers between devices with their start and end apart: 22 -> 21, of which waited for: 18 -> 13; matrix products, arithmetic and copies ran while one was open for 18% -> 17% of each run, Pallas kernels for 0% -> 0%
where the time goes in v1:
time: 1250 us
  waiting for transfers between devices  698 us (56%)
  blocking collectives  207 us (17%)
  matrix products  190 us (15%)
  local copies, waits for them, and re-layouts  77.8 us (6%)
  other arithmetic  48.6 us (4%)
  between operations  17.5 us (1%)
    reduce_scatter x2, waiting for transfers between devices, on_device(): lax.psum_scatter(product(context, out_whole), 'tensor', scatter_dimension...  160 us
    reduce_scatter x2, waiting for transfers between devices, on_device(): lax.psum_scatter(jnp.einsum('krx,kdx->rd', triple_half, in_whole, preferr...  152 us
    all_to_all x1, blocking collectives, on_device(): lax.all_to_all(jnp.stack([second_norm] * lax.axis_size('tensor')), 'tenso...  135 us
    all_to_all x1, waiting for transfers between devices, on_device(): lax.all_to_all(jnp.stack([second_norm] * lax.axis_size('tensor')), 'tenso...  107 us
    reduce_scatter x2, waiting for transfers between devices, on_device(): lax.psum_scatter(product(hidden, down_whole).astype(jnp.bfloat16), 'tenso...  83.6 us
    reduce_scatter x2, waiting for transfers between devices, on_device(): lax.psum_scatter(product_right_t(pre_half, up_whole), 'tensor', scatter_d...  60.4 us
    reduce_scatter x1, waiting for transfers between devices, on_device(): lax.psum_scatter(down_sum, 'fsdp', scatter_dimension=1, tiled=True)  43.7 us
    all_gather x2, waiting for transfers between devices, on_device(): first_full = lax.all_gather(first_norm, 'tensor', axis=0, tiled=True)  43.2 us
  transfers between devices with their start and end apart: 21, of which 13 were waited for; matrix products, arithmetic and copies ran while one was open for 17% of the time, Pallas kernels for 0%

profile of v1, /device:TPU:0, one launch (start us, length us, event | category | flops | bytes accessed | tf_op | source)
XLA Modules:
  0.0 1247.5 jit_solution(15103964849919905253)
XLA Ops:
  18.8 11.3 all-gather.2
  31.6 21.0 %all_gather.21 = bf16[3,1152,144]{2,0,1:T(4,128)(2,1)S(1)} all-gather(bf16[3,288,144]{2,0,1:T(4,128)(2,1)S(1)} %copy.40), channel_id=1, replica_groups=mesh['fsdp'=4,'tensor'=8] {'fsdp'}, dimensions={1}, use_global_device_ids=true | all-gather | bytes 1244160 | tf_op jit(solution)/shard_map/all_gather | solution.py:58
  52.6 3.2 copy.41
  55.8 5.0 all-gather.12.cloned.1.call-done
  60.8 4.2 fusion.173
  65.2 38.2 %all-gather.18.cloned.1.call-done = bf16[1536,1152]{1,0:T(8,128)(2,1)} async-done(((bf16[192,1152]{1,0:T(8,128)(2,1)}), bf16[1536,1152]{1,0:T(8,128)(2,1)}) %all-gather.18.cloned.1.call-update) | async-done | bytes 3538960 | tf_op jit(solution)/shard_map/all_gather | solution.py:196
  103.4 3.9 fusion.175
  116.7 13.7 %while.54 = (s32[]{:T(128)}, bf16[2,768,144]{1,2,0:T(8,128)(2,1)S(1)}, f32[2,2,768,1]{2,1,3,0:T(2,128)S(1)}, s32[2,768]{1,0:T(2,128)S(1)}, s32[1,1536]{1,0:T(1,1...) while((s32[]{:T(128)}, ...), condition=%wide.region_4.5_spmd, body=%wide.region_2.4_spmd.sunk | while | flops 697281024 | bytes 24247424 | solution.py:100
  117.5 3.1 select_reduce_fusion.4
  120.6 2.8 fusion.262
  124.3 3.1 select_reduce_fusion.4
  127.5 2.8 fusion.262
  131.2 4.2 fusion.174
  137.4 13.8 %while.55 = (s32[]{:T(128)}, bf16[2,768,144]{1,2,0:T(8,128)(2,1)S(1)}, f32[2,2,768,1]{2,1,3,0:T(2,128)S(1)}, s32[2,768]{1,0:T(2,128)S(1)}, s32[1,1536]{1,0:T(1,1...) while((s32[]{:T(128)}, ...), condition=%wide.region_13.14_spmd, body=%wide.region_11.13_spmd.sunk | while | flops 697281024 | bytes 24247424 | solution.py:100
  138.2 3.1 select_reduce_fusion.5
  141.3 2.9 fusion.265
  145.0 3.1 select_reduce_fusion.5
  148.2 2.9 fusion.265
  151.2 4.2 fusion.176
  157.8 53.8 %reduce-scatter.17.cloned.1.call-done = f32[192,1152]{1,0:T(8,128)} async-done(((f32[1536,1152]{1,0:T(8,128)}), f32[192,1152]{1,0:T(8,128)}) %reduce-scatter.17.cloned.1.call-update) | async-done | bytes 884752 | tf_op jit(solution)/shard_map/reduce_scatter | solution.py:204
  211.6 106.3 %reduce-scatter.21.cloned.1.call-done = f32[192,1152]{1,0:T(8,128)} async-done(((f32[1536,1152]{1,0:T(8,128)}), f32[192,1152]{1,0:T(8,128)}) %reduce-scatter.21.cloned.1.call-update) | async-done | bytes 884752 | tf_op jit(solution)/shard_map/reduce_scatter | solution.py:204
  323.5 4.6 all-to-all-start
  329.2 107.4 %all-to-all-done = bf16[8,192,1152]{2,1,0:T(8,128)(2,1)} async-done(((bf16[8,192,1152]{2,1,0:T(8,128)(2,1)}), bf16[8,192,1152]{2,1,0:T(8,128)(2,1)}, u32[]{:S(2)}, u32[]{:S(2)}) %all-to-all-start) | async-done | bytes 3538976 | tf_op jit(solution)/shard_map/all_to_all | solution.py:214
  436.5 6.5 convolution_add_fusion.3
  443.0 9.2 fusion.169
  453.4 5.3 fusion.146
  459.2 134.7 %all_to_all.10 = bf16[8,192,1152]{2,1,0:T(8,128)(2,1)S(1)} all-to-all(bf16[8,192,1152]{2,1,0:T(8,128)(2,1)S(1)} %stack.120), channel_id=1, replica_groups=mesh['fsdp'=4,'tensor'=8] {'tensor'}, dimensions={0} | all-to-all | bytes 7077888 | tf_op jit(solution)/shard_map/all_to_all | solution.py:214
  595.7 4.1 convolution_add_fusion.2
  599.8 9.3 fusion.170
  610.3 5.4 fusion.142
  616.1 7.6 convolution_convert_fusion.1
  623.8 7.6 convolution_convert_fusion
  631.6 60.3 %reduce-scatter.29.cloned.1.call-done = f32[192,1152]{1,0:T(8,128)} async-done(((f32[1536,1152]{1,0:T(8,128)}), f32[192,1152]{1,0:T(8,128)}) %reduce-scatter.29.cloned.1.call-update) | async-done | bytes 884752 | tf_op jit(solution)/shard_map/reduce_scatter | solution.py:235
  691.9 2.8 multiply_reduce_fusion.3
  696.9 39.3 %reduce-scatter.19.cloned.1.call-done = bf16[192,1152]{1,0:T(8,128)(2,1)} async-done(((bf16[1536,1152]{1,0:T(8,128)(2,1)}), bf16[192,1152]{1,0:T(8,128)(2,1)}) %reduce-scatter.19.cloned.1.call-update) | async-done | bytes 442384 | tf_op jit(solution)/shard_map/reduce_scatter | solution.py:219
  736.2 44.3 %reduce-scatter.23.cloned.1.call-done = bf16[192,1152]{1,0:T(8,128)(2,1)} async-done(((bf16[1536,1152]{1,0:T(8,128)(2,1)}), bf16[192,1152]{1,0:T(8,128)(2,1)}) %reduce-scatter.23.cloned.1.call-update) | async-done | bytes 442384 | tf_op jit(solution)/shard_map/reduce_scatter | solution.py:219
  780.6 4.4 fusion.156
  789.0 37.8 %all-gather.20.cloned.1.call-done = bf16[1536,1152]{1,0:T(8,128)(2,1)} async-done(((bf16[192,1152]{1,0:T(8,128)(2,1)}), bf16[1536,1152]{1,0:T(8,128)(2,1)}) %all-gather.20.cloned.1.call-update) | async-done | bytes 3538960 | tf_op jit(solution)/shard_map/all_gather | solution.py:242
  826.9 3.3 convolution_convert_fusion.3
  833.0 40.6 %while.56 = (s32[]{:T(128)}, f32[1536,2,72]{0,2,1:T(8,128)S(1)}, f32[1536,2,72]{0,2,1:T(8,128)}, f32[2,768,144]{1,2,0:T(8,128)}, bf16[2,768,2,72]{1,3,2,0:T(8,12...) while((s32[]{:T(128)}, f32[1536,2,72]{0,2,1:T(8,128)S(1)}, ...), condition=%wide.region_22.23_spmd.clone, body=%wide.region_21.22_spmd.clone.sunk | while | flops 1727150592 | bytes 81067536 | solution.py:148
  842.7 2.8 fusion.278
  845.5 4.1 multiply_convert_fusion.10
  863.0 2.8 fusion.278
  865.8 4.1 multiply_convert_fusion.10
  873.7 3.4 convolution_convert_fusion.2
  878.3 38.0 %while.57 = (s32[]{:T(128)}, f32[1536,2,72]{0,2,1:T(8,128)S(1)}, f32[1536,2,72]{0,2,1:T(8,128)}, f32[2,768,144]{1,2,0:T(8,128)}, bf16[2,768,2,72]{1,3,2,0:T(8,12...) while((s32[]{:T(128)}, f32[1536,2,72]{0,2,1:T(8,128)S(1)}, ...), condition=%wide.region_30.31_spmd.clone, body=%wide.region_29.30_spmd.clone.sunk | while | flops 1727150592 | bytes 77491600 | solution.py:148
  886.8 2.8 fusion.292
  889.6 4.1 multiply_convert_fusion.11
  905.6 2.8 fusion.292
  908.4 4.1 multiply_convert_fusion.11
  916.3 3.0 fusion.177
  934.6 4.0 copy.70
  938.6 6.3 reshape.427
  945.0 5.2 convolution_bitcast_fusion.3
  951.4 5.2 convolution_bitcast_fusion.2
  958.1 5.1 fusion.144
  963.2 4.6 convolution_add_fusion.1
  968.2 6.6 fusion.77
  974.8 4.8 convolution_add_fusion
  984.5 7.3 reduce-scatter.37.cloned.1.call-done
  996.8 74.2 %reduce-scatter.27.cloned.1.call-done = f32[192,1152]{1,0:T(8,128)} async-done(((f32[1536,1152]{1,0:T(8,128)}), f32[192,1152]{1,0:T(8,128)}) %reduce-scatter.27.cloned.1.call-update) | async-done | bytes 884752 | tf_op jit(solution)/shard_map/reduce_scatter | solution.py:259
  1071.0 77.9 %reduce-scatter.31.cloned.1.call-done = f32[192,1152]{1,0:T(8,128)} async-done(((f32[1536,1152]{1,0:T(8,128)}), f32[192,1152]{1,0:T(8,128)}) %reduce-scatter.31.cloned.1.call-update) | async-done | bytes 884752 | tf_op jit(solution)/shard_map/reduce_scatter | solution.py:259
  1151.4 39.9 %all-reduce = (f32[2,1152]{1,0:T(2,128)}, f32[4,1152]{1,0:T(4,128)}, f32[2,1152]{1,0:T(2,128)S(1)}, f32[4304]{0:T(1024)S(1)}) all-reduce(f32[2,1152]{1,0:T(2,128)S(1)} %maximum_add_fusion.1, f32[4,1152]{1,0:T(4,128)S(1)} %maximum_add_fusion, ...), channel_id=1, replica_groups=mesh['fsdp'=4,'tensor'=8] {'fsdp','tensor'}, use_global_device_ids=true, to_apply=%region_38.39 | all-reduce | flops 13520 | bytes 108160 | tf_op jit(solution)/shard_map/psum | solution.py:297
  1196.0 43.7 %reduce-scatter.35.cloned.1.call-done = f32[538,288]{0,1:T(8,128)} async-done(((f32[538,1152]{0,1:T(8,128)}), f32[538,288]{0,1:T(8,128)}) %reduce-scatter.35.cloned.1.call-update) | async-done | bytes 619792 | tf_op jit(solution)/shard_map/reduce_scatter | solution.py:286
  (489 shorter events, 136.5 us)
Async XLA Ops:
  8.0 9.3 copy-start.95
  8.0 9.5 copy-start.91
  8.0 10.7 copy-start.71
  8.0 23.2 %copy-start.60 = (bf16[3,288,144]{1,2,0:T(8,128)(2,1)S(1)}, bf16[3,288,144]{1,2,0:T(8,128)(2,1)}, u32[]{:S(2)}) copy-start(bf16[3,288,144]{1,2,0:T(8,128)(2,1)} %param.23) | copy-start | bytes 746500
  8.1 52.8 %all-gather.12.cloned.1.call-start = ((), (), s32[]{:S(2)}) async-start(), calls=%async_computation.14 | async-start | bytes 3981312 | tf_op jit(solution)/shard_map/all_gather | solution.py:196
  9.5 9.2 copy-start.79
  9.5 9.2 copy-start.81
  11.1 7.7 copy-start.85
  11.1 7.7 copy-start.87
  12.5 6.3 copy-start.68
  16.5 86.9 %all-gather.18.cloned.1.call-start = ((), (), s32[]{:S(2)}) async-start(), calls=%async_computation.19 | async-start | bytes 3981312 | tf_op jit(solution)/shard_map/all_gather | solution.py:196
  17.3 194.3 %reduce-scatter.17.cloned.1.call-start = ((), (), s32[]{:S(2)}) async-start(), calls=%async_computation.15 | async-start | bytes 7962624 | tf_op jit(solution)/shard_map/reduce_scatter | solution.py:204
  65.0 38.4 %copy-start.37 = (bf16[3,1152,144]{1,2,0:T(8,128)(2,1)S(1)}, bf16[3,1152,144]{1,2,0:T(8,128)(2,1)}, u32[]{:S(2)}) copy-start(bf16[3,1152,144]{1,2,0:T(8,128)(2,1)} %copy.41) | copy-start | bytes 2985988
  116.7 14.5 %copy-start.32 = (bf16[1152,144]{0,1:T(8,128)(2,1)S(1)}, bf16[1152,144]{0,1:T(8,128)(2,1)}, u32[]{:S(2)}) copy-start(bf16[1152,144]{0,1:T(8,128)(2,1)} %reshape.412) | copy-start | bytes 995332
  130.4 5.0 copy-start.6
  130.4 5.0 copy-start.67
  135.4 182.5 %reduce-scatter.21.cloned.1.call-start = ((), (), s32[]{:S(2)}) async-start(), calls=%async_computation.20 | async-start | bytes 7962624 | tf_op jit(solution)/shard_map/reduce_scatter | solution.py:204
  151.1 4.3 copy-start
  155.5 162.4 %copy-start.2 = (bf16[2,192,1152]{2,1,0:T(8,128)(2,1)S(1)}, bf16[2,192,1152]{2,1,0:T(8,128)(2,1)}, u32[]{:S(2)}) copy-start(bf16[2,192,1152]{2,1,0:T(8,128)(2,1)} %param.19) | copy-start | bytes 2654212
  155.5 173.6 %all-gather.14.cloned.1.call-start = ((), (), s32[]{:S(2)}) async-start(), calls=%async_computation.16 | async-start | bytes 1843200 | tf_op jit(solution)/shard_map/all_gather | solution.py:60
  156.1 286.9 %all-gather.16.cloned.1.call-start = ((), (), s32[]{:S(2)}) async-start(), calls=%async_computation.17 | async-start | bytes 1843200 | tf_op jit(solution)/shard_map/all_gather | solution.py:61
  156.7 286.3 %all-gather.24.cloned.1.call-start = ((), (), s32[]{:S(2)}) async-start(), calls=%async_computation.30 | async-start | bytes 3981312 | tf_op jit(solution)/shard_map/all_gather | solution.py:229
  157.7 162.5 %copy-start.70 = (f32[1152]{0:T(1024)S(1)}, f32[1152]{0:T(1024)}, u32[]{:S(2)}) copy-start(f32[1152]{0:T(1024)} %get-tuple-element.414) | copy-start | bytes 13828
  323.5 5.6 copy-start.94
  323.5 113.0 %all-to-all-start = ((bf16[8,192,1152]{2,1,0:T(8,128)(2,1)}), bf16[8,192,1152]{2,1,0:T(8,128)(2,1)}, u32[]{:S(2)}, u32[]{:S(2)}) async-start(bf16[8,192,1152]{2,1,0:T(8,128)(2,1)} %stack.118), calls=%async_computation.1 | async-start | bytes 7077888 | tf_op jit(solution)/shard_map/all_to_all | solution.py:214
  328.1 271.6 %all-gather.26.cloned.1.call-start = ((), (), s32[]{:S(2)}) async-start(), calls=%async_computation.31 | async-start | bytes 3981312 | tf_op jit(solution)/shard_map/all_gather | solution.py:229
  328.9 302.7 %reduce-scatter.25.cloned.1.call-start = ((), (), s32[]{:S(2)}) async-start(), calls=%async_computation.22 | async-start | bytes 7962624 | tf_op jit(solution)/shard_map/reduce_scatter | solution.py:235
  443.0 10.4 copy-start.99
  458.7 233.2 %reduce-scatter.29.cloned.1.call-start = ((), (), s32[]{:S(2)}) async-start(), calls=%async_computation.25 | async-start | bytes 7962624 | tf_op jit(solution)/shard_map/reduce_scatter | solution.py:235
  459.2 136.5 %copy-start.100 = (bf16[1152,538]{1,0:T(8,128)(2,1)S(1)}, bf16[1152,538]{1,0:T(8,128)(2,1)}, u32[]{:S(2)}) copy-start(bf16[1152,538]{1,0:T(8,128)(2,1)} %all-gather.14.cloned.1.call-done) | copy-start | bytes 3718660
  599.8 10.5 copy-start.101
  615.7 120.6 %reduce-scatter.19.cloned.1.call-start = ((), (), s32[]{:S(2)}) async-start(), calls=%async_computation.18 | async-start | bytes 3981312 | tf_op jit(solution)/shard_map/reduce_scatter | solution.py:219
  623.8 156.8 %reduce-scatter.23.cloned.1.call-start = ((), (), s32[]{:S(2)}) async-start(), calls=%async_computation.21 | async-start | bytes 3981312 | tf_op jit(solution)/shard_map/reduce_scatter | solution.py:219
  631.5 149.1 %copy-start.12 = (bf16[2,192,1152]{2,1,0:T(8,128)(2,1)S(1)}, bf16[2,192,1152]{2,1,0:T(8,128)(2,1)}, u32[]{:S(2)}) copy-start(bf16[2,192,1152]{2,1,0:T(8,128)(2,1)} %param.29) | copy-start | bytes 2654212
  631.5 195.4 %all-gather.20.cloned.1.call-start = ((), (), s32[]{:S(2)}) async-start(), calls=%async_computation.23 | async-start | bytes 3981312 | tf_op jit(solution)/shard_map/all_gather | solution.py:242
  785.0 41.9 %copy-start.33 = (bf16[1152,144]{0,1:T(8,128)(2,1)S(1)}, bf16[1152,144]{0,1:T(8,128)(2,1)}, u32[]{:S(2)}) copy-start(bf16[1152,144]{0,1:T(8,128)(2,1)} %reshape.412) | copy-start | bytes 995332
  786.7 87.0 %all-gather.22.cloned.1.call-start = ((), (), s32[]{:S(2)}) async-start(), calls=%async_computation.26 | async-start | bytes 3981312 | tf_op jit(solution)/shard_map/all_gather | solution.py:242
  788.8 193.9 %reduce-scatter.39.cloned.1.call-start = ((), (), s32[]{:S(2)}) async-start(), calls=%async_computation.33 | async-start | bytes 1474560
  873.7 4.6 copy-start.1
  873.7 4.6 copy-start.45
  873.7 4.6 copy-start.63
  873.7 4.6 copy-start.66
  919.6 4.3 copy-start.28
  923.7 68.0 %reduce-scatter.37.cloned.1.call-start = ((), (), s32[]{:S(2)}) async-start(), calls=%async_computation.32 | async-start | bytes 2949120
  927.0 5.5 copy-start.50
  927.7 4.7 copy-start.52
  938.6 6.4 copy-start.38
  938.6 6.4 copy-start.58
  944.9 126.1 %reduce-scatter.27.cloned.1.call-start = ((), (), s32[]{:S(2)}) async-start(), calls=%async_computation.24 | async-start | bytes 7962624 | tf_op jit(solution)/shard_map/reduce_scatter | solution.py:259
  950.2 198.8 %reduce-scatter.31.cloned.1.call-start = ((), (), s32[]{:S(2)}) async-start(), calls=%async_computation.27 | async-start | bytes 7962624 | tf_op jit(solution)/shard_map/reduce_scatter | solution.py:259
  956.6 239.4 %reduce-scatter.33.cloned.1.call-start = ((), (), s32[]{:S(2)}) async-start(), calls=%async_computation.28 | async-start | bytes 3686400 | tf_op jit(solution)/shard_map/reduce_scatter | solution.py:285
  958.1 5.1 copy-start.25
  958.1 5.1 copy-start.105
  967.9 271.8 %reduce-scatter.35.cloned.1.call-start = ((), (), s32[]{:S(2)}) async-start(), calls=%async_computation.29 | async-start | bytes 3686400 | tf_op jit(solution)/shard_map/reduce_scatter | solution.py:286
  968.1 6.7 copy-start.98
  968.1 6.7 copy-start.106
  980.8 168.1 %copy-start.3 = (bf16[2,192,1152]{2,1,0:T(8,128)(2,1)S(1)}, bf16[2,192,1152]{2,1,0:T(8,128)(2,1)}, u32[]{:S(2)}) copy-start(bf16[2,192,1152]{2,1,0:T(8,128)(2,1)} %param.19) | copy-start | bytes 2654212
  980.8 168.1 %copy-start.69 = (f32[1152]{0:T(1024)S(1)}, f32[1152]{0:T(1024)}, u32[]{:S(2)}) copy-start(f32[1152]{0:T(1024)} %copy-done.68) | copy-start | bytes 13828
  980.8 168.1 %copy-start.80 = (f32[192]{0:T(256)S(1)}, f32[192]{0:T(256)}, u32[]{:S(2)}) copy-start(f32[192]{0:T(256)} %copy-done.79) | copy-start | bytes 2308
  980.8 168.1 %copy-start.82 = (f32[192]{0:T(256)S(1)}, f32[192]{0:T(256)}, u32[]{:S(2)}) copy-start(f32[192]{0:T(256)} %copy-done.81) | copy-start | bytes 2308
  980.8 168.1 %copy-start.86 = (f32[192]{0:T(256)S(1)}, f32[192]{0:T(256)}, u32[]{:S(2)}) copy-start(f32[192]{0:T(256)} %copy-done.85) | copy-start | bytes 2308
  980.8 168.1 %copy-start.88 = (f32[192]{0:T(256)S(1)}, f32[192]{0:T(256)}, u32[]{:S(2)}) copy-start(f32[192]{0:T(256)} %copy-done.87) | copy-start | bytes 2308
  984.5 208.1 %copy-start.15 = (f32[192,1152]{1,0:T(8,128)S(1)}, f32[192,1152]{1,0:T(8,128)}, u32[]{:S(2)}) copy-start(f32[192,1152]{1,0:T(8,128)} %copy-done.14) | copy-start | bytes 2654212
  984.5 208.1 %copy-start.16 = (f32[192,1152]{1,0:T(8,128)S(1)}, f32[192,1152]{1,0:T(8,128)}, u32[]{:S(2)}) copy-start(f32[192,1152]{1,0:T(8,128)} %get-tuple-element.523) | copy-start | bytes 2654212
  (84 other events, 184.7 us)
Sparse Core Ops, SparseCore 0:
  16.6 44.1 all-gather.11
  63.1 40.2 all-gather.17
  135.5 75.9 reduce-scatter.16
  213.7 104.1 reduce-scatter.20
  786.8 39.9 all-gather.19
  828.9 40.2 all-gather.21
Sparse Core Ops, SparseCore 1:
  157.8 28.7 all-gather.13
  188.3 29.9 all-gather.15
  220.3 69.0 all-gather.23
  331.1 89.6 all-gather.25
  458.8 142.2 reduce-scatter.24
  615.7 76.1 reduce-scatter.28
  694.1 42.1 reduce-scatter.18
  738.4 42.1 reduce-scatter.22
  923.8 27.5 reduce-scatter.38
  954.4 37.3 reduce-scatter.36
  994.0 77.0 reduce-scatter.26
  1073.4 75.5 reduce-scatter.30
  1152.4 41.5 reduce-scatter.32
  1197.6 42.0 reduce-scatter.34
